TPU v7x, 1024 devices: a whole 8x8x8 slice. The times are simulated.
1024 devices in a mesh: gx: 32 (over x_hi, z, core), gy: 4 (over x_lo), gz: 8 (over y).
Axes of the slice: x: 8 (x_hi: 2, x_lo: 4; x = x_hi * 4 + x_lo), y: 8, z: 8, core: 2. Of those that a mesh axis runs over, the one named last changes fastest.
Arguments:
- density: float32 [128, 128, 1024], P('gx', 'gy', 'gz'), may hold values from 0.5 to 2
- velocity: float32 [3, 128, 128, 1024], P(None, 'gx', 'gy', 'gz'), may hold values from -2.5 to 2.5
- pressure: float32 [128, 128, 1024], P('gx', 'gy', 'gz'), may hold values from 0.5 to 2
Outputs:
- section_state: float32 [5, 128, 128, 1024], P(None, 'gx', 'gy', 'gz')
All inputs are finite; a program needn't handle non-finite values.
Results may differ from a plain program's by a relative error of at most 0.0003.
Values sent between devices are 32-bit elements; how exact they have to be, the bound alone decides.
A program may use at most 32 MiB of HBM per device.

v0:
```python
import functools

import jax
import jax.numpy as jnp
from jax import lax
from jax.sharding import Mesh
from jax.sharding import PartitionSpec as P

GX_GY_GZ = ("gx_0", "gx_1", "gx_2", "gy", "gz")
GX = ("gx_0", "gx_1", "gx_2")


gamma_gas = 1.4
weno_eps = 1e-06
cfl_number = 0.4


def over_axes(shard, axes):
    return functools.reduce(lax.pmax, axes, shard)


def padded_2(cells, sides, width):
    for axis, dim in sides:
        count = lax.axis_size(axis)
        head = lax.slice_in_dim(cells, 0, width, axis=dim)
        tail = lax.slice_in_dim(cells, cells.shape[dim] - width, cells.shape[dim], axis=dim)
        cells = jnp.concatenate(
            [
                lax.ppermute(tail, axis, [(i, (i + 1) % count) for i in range(count)]),
                cells,
                lax.ppermute(head, axis, [((i + 1) % count, i) for i in range(count)]),
            ],
            axis=dim,
        )
    return cells


def conserved(density, velocity, pressure):
    momenta = density[None] * velocity
    kinetic = 0.5 * density * jnp.sum(velocity * velocity, axis=0)
    energy = pressure / (gamma_gas - 1.0) + kinetic
    return jnp.concatenate([density[None], momenta, energy[None]], axis=0)


def wave_speed(density, velocity, pressure):
    sound = jnp.sqrt(gamma_gas * pressure / density)
    return jnp.max(jnp.sum(jnp.abs(velocity), axis=0) + 3.0 * sound)


def combine(coeffs, arrays):
    total = None
    for coeff, array in zip(coeffs, arrays):
        if isinstance(coeff, float) and coeff == 0.0:
            continue
        term = coeff * array
        total = term if total is None else total + term
    return total


def weno_face(values):
    first, second, third, fourth, fifth = values
    cand_left = (2.0 * first - 7.0 * second + 11.0 * third) / 6.0
    cand_middle = (-second + 5.0 * third + 2.0 * fourth) / 6.0
    cand_right = (2.0 * third + 5.0 * fourth - fifth) / 6.0
    smooth_left = (
        13.0 / 12.0 * (first - 2.0 * second + third) ** 2
        + 0.25 * (first - 4.0 * second + 3.0 * third) ** 2
    )
    smooth_middle = (
        13.0 / 12.0 * (second - 2.0 * third + fourth) ** 2 + 0.25 * (second - fourth) ** 2
    )
    smooth_right = (
        13.0 / 12.0 * (third - 2.0 * fourth + fifth) ** 2
        + 0.25 * (3.0 * third - 4.0 * fourth + fifth) ** 2
    )
    weight_left = 0.1 / (weno_eps + smooth_left) ** 2
    weight_middle = 0.6 / (weno_eps + smooth_middle) ** 2
    weight_right = 0.3 / (weno_eps + smooth_right) ** 2
    return (weight_left * cand_left + weight_middle * cand_middle + weight_right * cand_right) / (
        weight_left + weight_middle + weight_right
    )


def direction_flux(padded, field_dim, normal_comp):
    cells = padded.shape[field_dim + 1] - 6
    faces = cells + 1
    density = padded[0]
    energy = padded[4]
    velocity = [padded[1 + member] / density for member in range(3)]
    speed_sq = velocity[0] * velocity[0] + velocity[1] * velocity[1] + velocity[2] * velocity[2]
    pressure = (gamma_gas - 1.0) * (energy - 0.5 * density * speed_sq)
    sound_sq = gamma_gas * pressure / density
    sound = jnp.sqrt(sound_sq)
    enthalpy = (energy + pressure) / density
    normal_vel = velocity[normal_comp]
    others = [member for member in range(3) if member != normal_comp]
    order = [0, 1 + normal_comp, 1 + others[0], 1 + others[1], 4]
    state_perm = [padded[member] for member in order]
    flux_perm = [
        density * normal_vel,
        padded[1 + normal_comp] * normal_vel + pressure,
        padded[1 + others[0]] * normal_vel,
        padded[1 + others[1]] * normal_vel,
        (energy + pressure) * normal_vel,
    ]
    signal = jnp.abs(normal_vel) + sound

    def window(array, offset):
        return lax.slice_in_dim(array, offset, offset + faces, axis=field_dim)

    root_left = jnp.sqrt(window(density, 2))
    root_right = jnp.sqrt(window(density, 3))
    share_left = root_left / (root_left + root_right)
    share_right = root_right / (root_left + root_right)
    roe_vel = [
        share_left * window(member, 2) + share_right * window(member, 3) for member in velocity
    ]
    roe_enth = share_left * window(enthalpy, 2) + share_right * window(enthalpy, 3)
    jump_sq = sum(((window(member, 3) - window(member, 2)) ** 2 for member in velocity))
    roe_sound_sq = (
        share_left * window(sound_sq, 2)
        + share_right * window(sound_sq, 3)
        + 0.5 * (gamma_gas - 1.0) * share_left * share_right * jump_sq
    )
    roe_sound = jnp.sqrt(roe_sound_sq)
    normal_roe = roe_vel[normal_comp]
    tang_first = roe_vel[others[0]]
    tang_second = roe_vel[others[1]]
    roe_qsq = normal_roe * normal_roe + tang_first * tang_first + tang_second * tang_second
    b_one = (gamma_gas - 1.0) / roe_sound_sq
    b_two = 0.5 * b_one * roe_qsq
    inv_sound = 1.0 / roe_sound
    left_rows = [
        [
            0.5 * (b_two + normal_roe * inv_sound),
            -0.5 * (b_one * normal_roe + inv_sound),
            -0.5 * b_one * tang_first,
            -0.5 * b_one * tang_second,
            0.5 * b_one,
        ],
        [1.0 - b_two, b_one * normal_roe, b_one * tang_first, b_one * tang_second, -b_one],
        [-tang_first, 0.0, 1.0, 0.0, 0.0],
        [-tang_second, 0.0, 0.0, 1.0, 0.0],
        [
            0.5 * (b_two - normal_roe * inv_sound),
            -0.5 * (b_one * normal_roe - inv_sound),
            -0.5 * b_one * tang_first,
            -0.5 * b_one * tang_second,
            0.5 * b_one,
        ],
    ]
    right_rows = [
        [1.0, 1.0, 0.0, 0.0, 1.0],
        [normal_roe - roe_sound, normal_roe, 0.0, 0.0, normal_roe + roe_sound],
        [tang_first, tang_first, 1.0, 0.0, tang_first],
        [tang_second, tang_second, 0.0, 1.0, tang_second],
        [
            roe_enth - normal_roe * roe_sound,
            0.5 * roe_qsq,
            tang_first,
            tang_second,
            roe_enth + normal_roe * roe_sound,
        ],
    ]
    alpha = window(signal, 0)
    for offset in range(1, 6):
        alpha = jnp.maximum(alpha, window(signal, offset))
    plus_vals = [[None] * 6 for member in range(5)]
    minus_vals = [[None] * 6 for member in range(5)]
    for offset in range(6):
        state_here = [window(member, offset) for member in state_perm]
        flux_here = [window(member, offset) for member in flux_perm]
        for charac in range(5):
            char_state = combine(left_rows[charac], state_here)
            char_flux = combine(left_rows[charac], flux_here)
            plus_vals[charac][offset] = 0.5 * (char_flux + alpha * char_state)
            minus_vals[charac][offset] = 0.5 * (char_flux - alpha * char_state)
    hats = []
    for charac in range(5):
        upwind = weno_face(plus_vals[charac][0:5])
        downwind = weno_face(
            [
                minus_vals[charac][5],
                minus_vals[charac][4],
                minus_vals[charac][3],
                minus_vals[charac][2],
                minus_vals[charac][1],
            ]
        )
        hats.append(upwind + downwind)
    face_flux = [None] * 5
    for member in range(5):
        face_flux[order[member]] = combine(right_rows[member], hats)
    result = [
        lax.slice_in_dim(member, 1, faces, axis=field_dim)
        - lax.slice_in_dim(member, 0, faces - 1, axis=field_dim)
        for member in face_flux
    ]
    return jnp.stack(result, axis=0)


def local(density, velocity, pressure):
    state = conserved(density, velocity, pressure)
    local_top = wave_speed(density, velocity, pressure)
    top = over_axes(local_top, GX_GY_GZ)
    along_first = padded_2(state, ((GX, 1),), 3)
    along_second = padded_2(state, (("gy", 2),), 3)
    along_third = padded_2(state, (("gz", 3),), 3)
    total = direction_flux(along_first, 0, 0)
    total = total + direction_flux(along_second, 1, 1)
    total = total + direction_flux(along_third, 2, 2)
    step = cfl_number / top
    return state - step * total


def solution(mesh):
    split = Mesh(
        mesh.devices.reshape(2, 8, 2, mesh.shape["gy"], mesh.shape["gz"]),
        ("gx_0", "gx_1", "gx_2", "gy", "gz"),
    )
    return jax.shard_map(
        local,
        mesh=split,
        in_specs=(P(GX, "gy", "gz"), P(None, GX, "gy", "gz"), P(GX, "gy", "gz")),
        out_specs=P(None, GX, "gy", "gz"),
        check_vma=False,
    )
```

profile of v0, /device:TPU:1, one launch (start us, length us, event | category | flops | bytes accessed | tf_op | source)
XLA Modules:
  0.0 117.9 jit_solution(13079521110969262917)
XLA Ops:
  0.0 1.0 abs_reduce_fusion
  1.0 0.6 add_reduce_fusion
  1.7 0.2 fusion.149
  1.9 6.7 %collective-permute-start.5 = (f32[5,4,32,3]{3,2,1,0:T(8,128)S(1)}, f32[5,4,32,3]{3,2,1,0:T(8,128)S(1)}, u32[]{:S(2)}, u32[]{:S(2)}) collective-permute-start(f32[5,4,32,3]{3,2,1,0:T(8,128)S(1)} %get-tuple-element.103), channel_id=1, source_target_pairs={{1,0},{2,1},{3,2},{4,3},{5,4},{6,5},{7,6},{0,7},{9,8},{10,9},{11,1... | collective-permute-start | bytes 23048 | tf_op jit(solution)/shard_map/ppermute | solution.py:31
  8.6 1.9 %collective-permute-start.4 = (f32[5,4,32,3]{3,2,1,0:T(8,128)S(1)}, f32[5,4,32,3]{3,2,1,0:T(8,128)S(1)}, u32[]{:S(2)}, u32[]{:S(2)}) collective-permute-start(f32[5,4,32,3]{3,2,1,0:T(8,128)S(1)} %get-tuple-element.102), channel_id=1, source_target_pairs={{0,1},{1,2},{2,3},{3,4},{4,5},{5,6},{6,7},{7,0},{8,9},{9,10},{10,1... | collective-permute-start | bytes 23048 | tf_op jit(solution)/shard_map/ppermute | solution.py:29
  10.6 8.3 %pmax.35 = f32[]{:T(128)} all-reduce(f32[]{:T(128)} %get-tuple-element.116), channel_id=1, replica_groups=mesh['gx_0'=2,'gx_1'=8,'gx_2'=2,'gy'=4,'gz'=8] {'gx_0'}, use_global_device_ids=true, to_apply=%region_3.0 | all-reduce | flops 1 | bytes 8 | tf_op jit(solution)/shard_map/pmax | solution.py:19
  18.9 5.0 %collective-permute-start.3 = (f32[5,4,3,128]{3,2,1,0:T(4,128)S(1)}, f32[5,4,3,128]{3,2,1,0:T(4,128)S(1)}, u32[]{:S(2)}, u32[]{:S(2)}) collective-permute-start(f32[5,4,3,128]{3,2,1,0:T(4,128)S(1)} %get-tuple-element.97), channel_id=1, source_target_pairs={{8,0},{16,8},{24,16},{0,24},{9,1},{17,9},{25,17},{1,25},{10,2},{18... | collective-permute-start | bytes 92168 | tf_op jit(solution)/shard_map/ppermute | solution.py:31
  23.8 26.5 %pmax.36 = f32[]{:T(128)} all-reduce(f32[]{:T(128)} %pmax.35), channel_id=1, replica_groups=mesh['gx_0'=2,'gx_1'=8,'gx_2'=2,'gy'=4,'gz'=8] {'gx_1'}, use_global_device_ids=true, to_apply=%region_4.0 | all-reduce | flops 1 | bytes 8 | tf_op jit(solution)/shard_map/pmax | solution.py:19
  50.4 1.9 %collective-permute-start.2 = (f32[5,4,3,128]{3,2,1,0:T(4,128)S(1)}, f32[5,4,3,128]{3,2,1,0:T(4,128)S(1)}, u32[]{:S(2)}, u32[]{:S(2)}) collective-permute-start(f32[5,4,3,128]{3,2,1,0:T(4,128)S(1)} %get-tuple-element.96), channel_id=1, source_target_pairs={{0,8},{8,16},{16,24},{24,0},{1,9},{9,17},{17,25},{25,1},{2,10},{10... | collective-permute-start | bytes 92168 | tf_op jit(solution)/shard_map/ppermute | solution.py:29
  52.3 8.8 %pmax.37 = f32[]{:T(128)} all-reduce(f32[]{:T(128)} %pmax.36), channel_id=1, replica_groups=mesh['gx_0'=2,'gx_1'=8,'gx_2'=2,'gy'=4,'gz'=8] {'gx_2'}, use_global_device_ids=true, to_apply=%region_5.0 | all-reduce | flops 1 | bytes 8 | tf_op jit(solution)/shard_map/pmax | solution.py:19
  61.2 10.8 %pmax.38 = f32[]{:T(128)} all-reduce(f32[]{:T(128)} %pmax.37), channel_id=1, replica_groups=mesh['gx_0'=2,'gx_1'=8,'gx_2'=2,'gy'=4,'gz'=8] {'gy'}, use_global_device_ids=true, to_apply=%region_6.0 | all-reduce | flops 1 | bytes 8 | tf_op jit(solution)/shard_map/pmax | solution.py:19
  72.0 4.3 %collective-permute-start.1 = (f32[5,3,32,128]{3,2,1,0:T(8,128)S(1)}, f32[5,3,32,128]{3,2,1,0:T(8,128)S(1)}, u32[]{:S(2)}, u32[]{:S(2)}) collective-permute-start(f32[5,3,32,128]{3,2,1,0:T(8,128)S(1)} %get-tuple-element.101), channel_id=1, source_target_pairs={{32,0},{64,32},{96,64},{128,96},{160,128},{192,160},{224,192},{256... | collective-permute-start | bytes 737288 | tf_op jit(solution)/shard_map/ppermute | solution.py:31
  76.2 14.3 %pmax.39 = f32[]{:T(128)} all-reduce(f32[]{:T(128)} %pmax.38), channel_id=1, replica_groups=mesh['gx_0'=2,'gx_1'=8,'gx_2'=2,'gy'=4,'gz'=8] {'gz'}, use_global_device_ids=true, to_apply=%region_7.0 | all-reduce | flops 1 | bytes 8 | tf_op jit(solution)/shard_map/pmax | solution.py:19
  91.2 5.0 %collective-permute-start = (f32[5,3,32,128]{3,2,1,0:T(8,128)S(1)}, f32[5,3,32,128]{3,2,1,0:T(8,128)S(1)}, u32[]{:S(2)}, u32[]{:S(2)}) collective-permute-start(f32[5,3,32,128]{3,2,1,0:T(8,128)S(1)} %get-tuple-element.100), channel_id=1, source_target_pairs={{0,32},{32,64},{64,96},{96,128},{128,160},{160,192},{192,224},{224... | collective-permute-start | bytes 737288 | tf_op jit(solution)/shard_map/ppermute | solution.py:29
  96.3 0.3 pad_maximum_fusion.1
  96.6 0.1 fusion.120
  96.7 0.2 add_divide_fusion.1
  96.9 0.1 fusion.129
  97.0 9.1 %multiply_add_fusion.3 = (f32[4,32,129]{2,1,0:T(8,128)S(1)}, f32[4,32,129]{2,1,0:T(8,128)S(1)}, f32[4,32,129]{2,1,0:T(8,128)S(1)}, f32[4,32,129]{2,1,0:T(8,128)S...) fusion(f32[4,32,129]{2,1,0:T(8,128)S(1)} %get-tuple-element.119, ...), kind=kLoop, calls=%fused_computation.47 | loop fusion | flops 18889728 | bytes 5812224 | tf_op jit(solution)/shard_map/add | solution.py:56
  106.1 0.1 multiply_add_fusion.4
  106.4 0.1 fusion.96
  106.5 0.1 fusion.94
  106.5 0.1 fusion.92
  107.0 4.6 %multiply_add_fusion.15 = (f32[4,33,128]{2,1,0:T(8,128)S(1)}, f32[4,33,128]{2,1,0:T(8,128)S(1)}, f32[4,33,128]{2,1,0:T(8,128)S(1)}, f32[4,33,128]{2,1,0:T(8,128)...) fusion(f32[4,33,128]{2,1,0:T(8,128)S(1)} %get-tuple-element.121, ...), kind=kLoop, calls=%fused_computation.207 | loop fusion | flops 19329024 | bytes 5947392 | tf_op jit(solution)/shard_map/add | solution.py:56
  111.7 0.1 fusion.90
  111.9 0.1 fusion.27
  112.0 0.1 multiply_add_fusion
  112.1 0.1 maximum_maximum_fusion
  112.3 0.1 fusion.34
  112.4 4.4 %multiply_add_fusion.22 = (f32[5,32,128]{2,1,0:T(8,128)S(1)}, f32[5,32,128]{2,1,0:T(8,128)S(1)}, f32[5,32,128]{2,1,0:T(8,128)S(1)}, f32[5,32,128]{2,1,0:T(8,128)...) fusion(f32[5,32,128]{2,1,0:T(8,128)S(1)} %get-tuple-element.115, f32[5,32,128]{2,1,0:T(8,128)S(1)} %get-tuple-element.114, ...), kind=kLoop, calls=%fused_computation.253 | loop fusion | flops 22937600 | bytes 6553600 | tf_op jit(solution)/shard_map/add | solution.py:56
  116.8 0.1 fusion.37
  117.0 0.9 multiply_subtract_fusion
  (32 shorter events, 0.8 us)
Async XLA Ops:
  0.0 1.0 copy-start
  0.0 1.0 copy-start.1
  1.9 89.3 %collective-permute-start.5 = (f32[5,4,32,3]{3,2,1,0:T(8,128)S(1)}, f32[5,4,32,3]{3,2,1,0:T(8,128)S(1)}, u32[]{:S(2)}, u32[]{:S(2)}) collective-permute-start(f32[5,4,32,3]{3,2,1,0:T(8,128)S(1)} %get-tuple-element.103), channel_id=1, source_target_pairs={{1,0},{2,1},{3,2},{4,3},{5,4},{6,5},{7,6},{0,7},{9,8},{10,9},{11,1... | collective-permute-start | bytes 23048 | tf_op jit(solution)/shard_map/ppermute | solution.py:31
  8.6 87.6 %collective-permute-start.4 = (f32[5,4,32,3]{3,2,1,0:T(8,128)S(1)}, f32[5,4,32,3]{3,2,1,0:T(8,128)S(1)}, u32[]{:S(2)}, u32[]{:S(2)}) collective-permute-start(f32[5,4,32,3]{3,2,1,0:T(8,128)S(1)} %get-tuple-element.102), channel_id=1, source_target_pairs={{0,1},{1,2},{2,3},{3,4},{4,5},{5,6},{6,7},{7,0},{8,9},{9,10},{10,1... | collective-permute-start | bytes 23048 | tf_op jit(solution)/shard_map/ppermute | solution.py:29
  18.9 87.8 %collective-permute-start.3 = (f32[5,4,3,128]{3,2,1,0:T(4,128)S(1)}, f32[5,4,3,128]{3,2,1,0:T(4,128)S(1)}, u32[]{:S(2)}, u32[]{:S(2)}) collective-permute-start(f32[5,4,3,128]{3,2,1,0:T(4,128)S(1)} %get-tuple-element.97), channel_id=1, source_target_pairs={{8,0},{16,8},{24,16},{0,24},{9,1},{17,9},{25,17},{1,25},{10,2},{18... | collective-permute-start | bytes 92168 | tf_op jit(solution)/shard_map/ppermute | solution.py:31
  50.4 56.3 %collective-permute-start.2 = (f32[5,4,3,128]{3,2,1,0:T(4,128)S(1)}, f32[5,4,3,128]{3,2,1,0:T(4,128)S(1)}, u32[]{:S(2)}, u32[]{:S(2)}) collective-permute-start(f32[5,4,3,128]{3,2,1,0:T(4,128)S(1)} %get-tuple-element.96), channel_id=1, source_target_pairs={{0,8},{8,16},{16,24},{24,0},{1,9},{9,17},{17,25},{25,1},{2,10},{10... | collective-permute-start | bytes 92168 | tf_op jit(solution)/shard_map/ppermute | solution.py:29
  72.0 39.8 %collective-permute-start.1 = (f32[5,3,32,128]{3,2,1,0:T(8,128)S(1)}, f32[5,3,32,128]{3,2,1,0:T(8,128)S(1)}, u32[]{:S(2)}, u32[]{:S(2)}) collective-permute-start(f32[5,3,32,128]{3,2,1,0:T(8,128)S(1)} %get-tuple-element.101), channel_id=1, source_target_pairs={{32,0},{64,32},{96,64},{128,96},{160,128},{192,160},{224,192},{256... | collective-permute-start | bytes 737288 | tf_op jit(solution)/shard_map/ppermute | solution.py:31
  91.2 20.6 %collective-permute-start = (f32[5,3,32,128]{3,2,1,0:T(8,128)S(1)}, f32[5,3,32,128]{3,2,1,0:T(8,128)S(1)}, u32[]{:S(2)}, u32[]{:S(2)}) collective-permute-start(f32[5,3,32,128]{3,2,1,0:T(8,128)S(1)} %get-tuple-element.100), channel_id=1, source_target_pairs={{0,32},{32,64},{64,96},{96,128},{128,160},{160,192},{192,224},{224... | collective-permute-start | bytes 737288 | tf_op jit(solution)/shard_map/ppermute | solution.py:29
where the time goes:
time: 118 us
  blocking collectives  68.7 us (58%)
  starting transfers between devices  24.8 us (21%)
  other arithmetic  22.9 us (19%)
    pmax x5, blocking collectives, over_axes(): return functools.reduce(lax.pmax, axes, shard)  68.7 us
    add x6, other arithmetic, combine(): total = term if total is None else total + term  18.3 us
    ppermute x3, starting transfers between devices, padded_2(): lax.ppermute(head, axis, [((i + 1) % count, i) for i in range(count)])  15.9 us
    ppermute x3, starting transfers between devices, padded_2(): lax.ppermute(tail, axis, [(i, (i + 1) % count) for i in range(count)])  8.88 us
  transfers between devices with their start and end apart: 6, of which 0 were waited for; matrix products, arithmetic and copies ran while one was open for 13% of the time, Pallas kernels for 0%

commit v1 on v0

v1 whole, which is shorter than its diff:
```python
import jax
import jax.numpy as jnp
from jax import lax
from jax.experimental import pallas as pl
from jax.experimental.pallas import tpu as pltpu
from jax.sharding import PartitionSpec as P

gamma_gas = 1.4
weno_eps = 1e-06
cfl_number = 0.4

MESH = pl.DeviceIdType.MESH

U0, UN, UA, UB, UE, FN, FA, FB, FE, ROOT, VN, VA, VB, ENTH, SOUND, SIGNAL = range(16)
ORDER = ((0, 1, 2), (1, 0, 2), (2, 0, 1))


def cell_values(density, normal, first, second, pressure):
    inv = 1.0 / density
    sound_sq = gamma_gas * pressure * inv
    sound = jnp.sqrt(sound_sq)
    half_sq = 0.5 * (normal * normal + first * first + second * second)
    energy = pressure * (1.0 / (gamma_gas - 1.0)) + density * half_sq
    total = energy + pressure
    mom_n = density * normal
    values = [None] * 16
    values[U0] = density
    values[UN] = mom_n
    values[UA] = density * first
    values[UB] = density * second
    values[UE] = energy
    values[FN] = mom_n * normal + pressure
    values[FA] = mom_n * first
    values[FB] = mom_n * second
    values[FE] = total * normal
    values[ROOT] = jnp.sqrt(density)
    values[VN] = normal
    values[VA] = first
    values[VB] = second
    values[ENTH] = total * inv
    values[SOUND] = sound_sq
    values[SIGNAL] = jnp.abs(normal) + sound
    return values, sound


def weno_part(d0, d1, d2, d3, eps):
    s1 = d1 - d0
    s2 = d2 - d1
    s3 = d3 - d2
    f1 = 0.75 * d1
    f2 = 0.75 * d2
    b0 = s1 * s1 + f1 * (d1 + s1) + eps
    b1 = s2 * s2 + f1 * d2 + eps
    b2 = s3 * s3 + f2 * (d2 - s3) + eps
    g0 = b1 * b2
    g1 = b0 * b2
    g2 = b0 * b1
    w0 = g0 * g0
    w1 = g1 * g1
    w2 = 3.0 * (g2 * g2)
    total = w0 + 6.0 * w1 + w2
    top = 2.0 * (w0 * (s1 - s2)) + w2 * (s2 - s3)
    return top / total


def face_block(load):
    alpha = load(SIGNAL, 0)
    for k in range(1, 6):
        alpha = jnp.maximum(alpha, load(SIGNAL, k))
    root_l = load(ROOT, 2)
    root_r = load(ROOT, 3)
    inv_sum = 1.0 / (root_l + root_r)
    wl = root_l * inv_sum
    wr = root_r * inv_sum
    vel = []
    jump_sq = None
    for member in (VN, VA, VB):
        left, right = load(member, 2), load(member, 3)
        vel.append(wl * left + wr * right)
        jump = right - left
        jump_sq = jump * jump if jump_sq is None else jump_sq + jump * jump
    un, ta, tb = vel
    enth = wl * load(ENTH, 2) + wr * load(ENTH, 3)
    sound_sq = (
        wl * load(SOUND, 2)
        + wr * load(SOUND, 3)
        + (0.5 * (gamma_gas - 1.0)) * (wl * wr) * jump_sq
    )
    sound = jnp.sqrt(sound_sq)
    inv_sound = 1.0 / sound
    b_one = (gamma_gas - 1.0) * inv_sound * inv_sound
    half_sq = 0.5 * (un * un + ta * ta + tb * tb)

    plus = [[None] * 5 for _ in range(4)]
    minus = [[None] * 5 for _ in range(4)]
    linear = []
    for comp in range(5):
        state = [load(U0 + comp, k) for k in range(6)]
        flux = [load(UN if comp == 0 else FN + comp - 1, k) for k in range(6)]
        for k in range(5):
            df = flux[k + 1] - flux[k]
            du = alpha * (state[k + 1] - state[k])
            if k < 4:
                plus[k][comp] = df + du
            if k > 0:
                minus[k - 1][comp] = df - du
        linear.append(
            6.0 * (flux[2] + flux[3])
            + ((plus[1][comp] - minus[2][comp]) + (minus[1][comp] - plus[2][comp]))
        )

    def project(vector):
        r, n, a, b, e = vector
        n_rel = n - un * r
        a_rel = a - ta * r
        b_rel = b - tb * r
        inner = e - (un * n_rel + ta * a_rel + tb * b_rel + half_sq * r)
        press = b_one * inner
        wave = n_rel * inv_sound
        return press - wave, r - press, a_rel, b_rel, press + wave

    plus = [project(vector) for vector in plus]
    minus = [project(vector) for vector in minus]
    hats = []
    for charac in range(5):
        scale = 16.0 if charac in (0, 4) else 4.0
        eps = 0.75 * scale * weno_eps
        up = weno_part(*(plus[k][charac] for k in (0, 1, 2, 3)), eps)
        down = weno_part(*(minus[k][charac] for k in (3, 2, 1, 0)), eps)
        hats.append(up - down)
    both = 0.5 * (hats[0] + hats[4])
    split = (0.5 * sound) * (hats[4] - hats[0])
    dens = both + hats[1]
    return [
        linear[0] + dens,
        linear[1] + (un * dens + split),
        linear[2] + (ta * dens + hats[2]),
        linear[3] + (tb * dens + hats[3]),
        linear[4]
        + (enth * both + un * split + half_sq * hats[1] + ta * hats[2] + tb * hats[3]),
    ]


def peers():
    gx = lax.axis_index("gx")
    gy = lax.axis_index("gy")
    gz = lax.axis_index("gz")
    core = gx % 2
    z = (gx // 2) % 8
    x_hi = gx // 16

    def at(x_hi, gy, z, core, gz):
        return {"gx": x_hi * 16 + z * 2 + core, "gy": gy, "gz": gz}

    lines = [[], [], []]
    for step in range(8):
        for flip in range(2):
            if step or flip:
                lines[0].append(at(x_hi, gy, z, (core + flip) % 2, (gz + step) % 8))
    for step in range(1, 8):
        lines[1].append(at(x_hi, gy, (z + step) % 8, core, gz))
    for step in range(1, 8):
        x = (x_hi * 4 + gy + step) % 8
        lines[2].append(at(x // 4, x % 4, z, core, gz))
    halos = []
    for shift in (1, -1):
        halos.append(
            (
                {"gx": (gx + shift + 32) % 32, "gy": gy, "gz": gz},
                {"gx": gx, "gy": (gy + shift + 4) % 4, "gz": gz},
                {"gx": gx, "gy": gy, "gz": (gz + shift + 8) % 8},
            )
        )
    far = {"gx": (gx + 31 + 2 * core) % 32, "gy": gy, "gz": gz}
    return lines, halos, far


def kernel(
    dens_ref,
    vel_ref,
    pres_ref,
    out_ref,
    raw_x,
    raw_y,
    raw_z,
    cell_x,
    cell_y,
    cell_z,
    flux_x,
    flux_y,
    flux_z,
    total,
    tops,
    top_in,
    load_sem,
    max_send,
    max_recv,
    halo_send,
    halo_recv,
):
    lines, halos, far = peers()
    barrier = pltpu.get_barrier_semaphore()
    loads = [
        pltpu.make_async_copy(dens_ref, raw_x.at[0, pl.ds(96, 128)], load_sem.at[0]),
        pltpu.make_async_copy(vel_ref.at[0], raw_x.at[1, pl.ds(96, 128)], load_sem.at[1]),
        pltpu.make_async_copy(vel_ref.at[1], raw_x.at[2, pl.ds(96, 128)], load_sem.at[2]),
        pltpu.make_async_copy(vel_ref.at[2], raw_x.at[3, pl.ds(96, 128)], load_sem.at[3]),
        pltpu.make_async_copy(pres_ref, raw_x.at[4, pl.ds(96, 128)], load_sem.at[4]),
    ]
    for copy in loads:
        copy.start()
    greeted = lines[0] + lines[1] + lines[2] + [far]
    for device in greeted:
        pl.semaphore_signal(barrier, inc=1, device_id=device, device_id_type=MESH)
    for copy in loads:
        copy.wait()

    def cells(raw, cell, direction, start, blocks):
        first, second, third = ORDER[direction]

        def body(block, carry):
            rows = pl.ds(pl.multiple_of(start + 8 * block, 8), 8)
            values, sound = cell_values(
                raw[0, rows, :],
                raw[1 + first, rows, :],
                raw[1 + second, rows, :],
                raw[1 + third, rows, :],
                raw[4, rows, :],
            )
            for index, value in enumerate(values):
                cell[index, rows, :] = value
            speed = (
                jnp.abs(values[VN]) + jnp.abs(values[VA]) + jnp.abs(values[VB]) + 3.0 * sound
            )
            return jnp.maximum(carry, speed)

        return lax.fori_loop(0, blocks, body, jnp.zeros((8, 128), jnp.float32))

    def faces(cell, flux, stride, start, blocks):
        def body(block, carry):
            base = pl.multiple_of(start + 8 * block, 8)

            def load(index, k):
                return cell[index, pl.ds(base + (k - 2) * stride, 8), :]

            for comp, value in enumerate(face_block(load)):
                flux[comp, pl.ds(base, 8), :] = value
            return carry

        lax.fori_loop(0, blocks, body, 0)

    local = cells(raw_x, cell_x, 0, 96, 16)
    tops[0] = jnp.max(local, axis=0, keepdims=True)

    for field in range(5):
        for x in range(4):
            for part in range(4):
                raw_y[field, pl.ds(16 + 32 * part + x, 8, stride=4), :] = raw_x[
                    field, pl.ds(96 + 32 * x + 8 * part, 8), :
                ]
        raw_z[field, pl.ds(16, 128), :] = raw_x[field, pl.ds(96, 128), :].T

    pl.semaphore_wait(barrier, len(greeted))

    def send_tops(phase):
        first = (0, 15, 22)[phase]
        copies = []
        for slot, device in enumerate(lines[phase]):
            copies.append(
                pltpu.make_async_remote_copy(
                    src_ref=tops.at[phase],
                    dst_ref=top_in.at[first + slot],
                    send_sem=max_send.at[first + slot],
                    recv_sem=max_recv.at[first + slot],
                    device_id=device,
                    device_id_type=MESH,
                )
            )
        for copy in copies:
            copy.start()
        return copies

    def gather_tops(phase, copies):
        first = (0, 15, 22)[phase]
        for copy in copies:
            copy.wait()
        top = tops[phase]
        for slot in range(len(copies)):
            top = jnp.maximum(top, top_in[first + slot])
        return top

    top_copies = send_tops(0)

    def send_halos(direction):
        raw, tail, tail_to, head, head_to, size = (
            (raw_x, 128, 0, 96, 224, 96),
            (raw_y, 128, 0, 16, 144, 16),
            (raw_z, 136, 8, 16, 144, 8),
        )[direction]
        copies = []
        for side, (source, target) in enumerate(((tail, tail_to), (head, head_to))):
            copies.append(
                pltpu.make_async_remote_copy(
                    src_ref=raw.at[:, pl.ds(source, size)],
                    dst_ref=raw.at[:, pl.ds(target, size)],
                    send_sem=halo_send.at[2 * direction + side],
                    recv_sem=halo_recv.at[2 * direction + side],
                    device_id=halos[side][direction],
                    device_id_type=MESH,
                )
            )
        for copy in copies:
            copy.start()
        return copies

    halo_z = send_halos(2)
    halo_y = send_halos(1)
    halo_x = send_halos(0)

    cells(raw_z, cell_z, 2, 16, 16)
    cells(raw_y, cell_y, 1, 16, 16)

    for copy in halo_z:
        copy.wait()
    cells(raw_z, cell_z, 2, 8, 1)
    cells(raw_z, cell_z, 2, 144, 1)
    faces(cell_z, flux_z, 1, 8, 17)

    tops[1] = gather_tops(0, top_copies)
    top_copies = send_tops(1)

    for copy in halo_y:
        copy.wait()
    cells(raw_y, cell_y, 1, 0, 2)
    cells(raw_y, cell_y, 1, 144, 2)
    faces(cell_y, flux_y, 4, 8, 17)

    tops[2] = gather_tops(1, top_copies)
    top_copies = send_tops(2)

    for comp in range(5):
        along_z = flux_z[comp_at(2, comp), pl.ds(16, 128), :] - flux_z[
            comp_at(2, comp), pl.ds(15, 128), :
        ]
        total[comp] = along_z.T
        along_y = comp_at(1, comp)
        for part in range(16):
            rows = pl.ds(16 + 8 * part, 8)
            flux_x[0, rows, :] = (
                flux_y[along_y, rows, :] - flux_y[along_y, pl.ds(12 + 8 * part, 8), :]
            )
        for x in range(4):
            for part in range(4):
                rows = pl.ds(32 * x + 8 * part, 8)
                total[comp, rows, :] = (
                    total[comp, rows, :]
                    + flux_x[0, pl.ds(16 + 32 * part + x, 8, stride=4), :]
                )

    for copy in halo_x:
        copy.wait()
    cells(raw_x, cell_x, 0, 0, 12)
    cells(raw_x, cell_x, 0, 224, 12)
    faces(cell_x, flux_x, 32, 64, 20)

    top = gather_tops(2, top_copies)
    step = (cfl_number / 12.0) / jnp.max(top, axis=1, keepdims=True)
    for comp in range(5):
        for part in range(16):
            rows = pl.ds(8 * part, 8)
            change = total[comp, rows, :] + (
                flux_x[comp, pl.ds(96 + 8 * part, 8), :]
                - flux_x[comp, pl.ds(64 + 8 * part, 8), :]
            )
            out_ref[comp, rows, :] = cell_x[comp, pl.ds(96 + 8 * part, 8), :] - step * change


def comp_at(direction, comp):
    if comp in (0, 4):
        return comp
    return 1 + ORDER[direction].index(comp - 1)


def local(density, velocity, pressure):
    f32 = jnp.float32
    result = pl.pallas_call(
        kernel,
        name="section",
        out_shape=jax.ShapeDtypeStruct((5, 128, 128), f32),
        in_specs=[pl.BlockSpec(memory_space=pltpu.HBM)] * 3,
        out_specs=pl.BlockSpec(memory_space=pltpu.VMEM),
        scratch_shapes=[
            pltpu.VMEM((5, 320, 128), f32),
            pltpu.VMEM((5, 160, 128), f32),
            pltpu.VMEM((5, 160, 128), f32),
            pltpu.VMEM((16, 320, 128), f32),
            pltpu.VMEM((16, 160, 128), f32),
            pltpu.VMEM((16, 160, 128), f32),
            pltpu.VMEM((5, 224, 128), f32),
            pltpu.VMEM((5, 144, 128), f32),
            pltpu.VMEM((5, 144, 128), f32),
            pltpu.VMEM((5, 128, 128), f32),
            pltpu.VMEM((3, 1, 128), f32),
            pltpu.VMEM((29, 1, 128), f32),
            pltpu.SemaphoreType.DMA((5,)),
            pltpu.SemaphoreType.DMA((29,)),
            pltpu.SemaphoreType.DMA((29,)),
            pltpu.SemaphoreType.DMA((6,)),
            pltpu.SemaphoreType.DMA((6,)),
        ],
        compiler_params=pltpu.CompilerParams(collective_id=0, has_side_effects=True),
    )(
        density.reshape(128, 128),
        velocity.reshape(3, 128, 128),
        pressure.reshape(128, 128),
    )
    return result.reshape(5, 4, 32, 128)


def solution(mesh):
    return jax.shard_map(
        local,
        mesh=mesh,
        in_specs=(P("gx", "gy", "gz"), P(None, "gx", "gy", "gz"), P("gx", "gy", "gz")),
        out_specs=P(None, "gx", "gy", "gz"),
        check_vma=False,
    )
```

time: 118 us -> 41.1 us (0.35)
  the two profiles are of different devices: /device:TPU:1 before, /device:TPU:2 now
where the time goes in v1:
time: 41.1 us; the launch traced here: 40.9 us
  Pallas kernels  39.1 us (95%)
  local copies, waits for them, and re-layouts  1.72 us (4%)
    pallas_call x1, Pallas kernels, local(): pl.pallas_call(kernel, name='section', out_shape=jax.ShapeDtypeStruct((5,...  39.1 us
    unnamed x1, local copies, waits for them, and re-layouts  1.72 us

profile of v1, /device:TPU:2, one launch (start us, length us, event | category | flops | bytes accessed | tf_op | source)
XLA Modules:
  0.0 40.9 jit_solution(18169010173232921357)
XLA Ops:
  0.0 39.1 %section.1 = f32[5,128,128]{2,1,0:T(8,128)} custom-call(f32[128,128]{1,0:T(8,128)} %bitcast.6, f32[3,128,128]{2,1,0:T(8,128)} %bitcast.5, f32[128,128]{1,0:T(8,128)} %bitcast.7), custom_call_target="tpu_custom_call" | custom-call | tf_op jit(solution)/shard_map/section/pallas_call | solution.py:386
  39.1 1.7 %copy.5 = f32[5,4,32,128]{3,2,1,0:T(8,128)} copy(f32[5,4,32,128]{3,2,1,0:T(8,128)} %bitcast.4) | data formatting | bytes 655360

commit v2 on v1

--- a/solution.py
+++ b/solution.py
@@ -40,7 +40,7 @@
     values[ENTH] = total * inv
     values[SOUND] = sound_sq
     values[SIGNAL] = jnp.abs(normal) + sound
-    return values, sound
+    return values
 
 
 def weno_part(d0, d1, d2, d3, eps):
@@ -141,38 +141,32 @@
     ]
 
 
-def peers():
+def place_of():
     gx = lax.axis_index("gx")
-    gy = lax.axis_index("gy")
-    gz = lax.axis_index("gz")
-    core = gx % 2
-    z = (gx // 2) % 8
-    x_hi = gx // 16
-
-    def at(x_hi, gy, z, core, gz):
-        return {"gx": x_hi * 16 + z * 2 + core, "gy": gy, "gz": gz}
-
-    lines = [[], [], []]
-    for step in range(8):
-        for flip in range(2):
-            if step or flip:
-                lines[0].append(at(x_hi, gy, z, (core + flip) % 2, (gz + step) % 8))
-    for step in range(1, 8):
-        lines[1].append(at(x_hi, gy, (z + step) % 8, core, gz))
-    for step in range(1, 8):
-        x = (x_hi * 4 + gy + step) % 8
-        lines[2].append(at(x // 4, x % 4, z, core, gz))
-    halos = []
+    return gx % 2, (gx // 2) % 8, (gx // 16) * 4 + lax.axis_index("gy"), lax.axis_index("gz")
+
+
+def device(core, place, across, gz):
+    return {"gx": (across // 4) * 16 + place * 2 + core, "gy": across % 4, "gz": gz}
+
+
+def neighbours():
+    gx, gy, gz = (lax.axis_index(name) for name in ("gx", "gy", "gz"))
+    found = []
     for shift in (1, -1):
-        halos.append(
+        found.append(
             (
                 {"gx": (gx + shift + 32) % 32, "gy": gy, "gz": gz},
                 {"gx": gx, "gy": (gy + shift + 4) % 4, "gz": gz},
                 {"gx": gx, "gy": gy, "gz": (gz + shift + 8) % 8},
             )
         )
-    far = {"gx": (gx + 31 + 2 * core) % 32, "gy": gy, "gz": gz}
-    return lines, halos, far
+    return found
+
+
+STEPS = [(i, j) for i in range(8) for j in range(8) if i or j]
+STEPS.sort(key=lambda ij: -min(ij[0], 8 - ij[0]) - min(ij[1], 8 - ij[1]))
+PLANE, FINAL = 16, 16 + 63
 
 
 def kernel(
@@ -198,29 +192,62 @@
     halo_send,
     halo_recv,
 ):
-    lines, halos, far = peers()
-    barrier = pltpu.get_barrier_semaphore()
+    core, place, across, gz = place_of()
+    first_place = place == 0
+    other_place = place != 0
+    early = place < 4
     loads = [
         pltpu.make_async_copy(dens_ref, raw_x.at[0, pl.ds(96, 128)], load_sem.at[0]),
+        pltpu.make_async_copy(pres_ref, raw_x.at[4, pl.ds(96, 128)], load_sem.at[4]),
         pltpu.make_async_copy(vel_ref.at[0], raw_x.at[1, pl.ds(96, 128)], load_sem.at[1]),
         pltpu.make_async_copy(vel_ref.at[1], raw_x.at[2, pl.ds(96, 128)], load_sem.at[2]),
         pltpu.make_async_copy(vel_ref.at[2], raw_x.at[3, pl.ds(96, 128)], load_sem.at[3]),
-        pltpu.make_async_copy(pres_ref, raw_x.at[4, pl.ds(96, 128)], load_sem.at[4]),
     ]
     for copy in loads:
         copy.start()
-    greeted = lines[0] + lines[1] + lines[2] + [far]
-    for device in greeted:
-        pl.semaphore_signal(barrier, inc=1, device_id=device, device_id_type=MESH)
+
+    barrier = pltpu.get_barrier_semaphore()
+
+    def greet(to):
+        pl.semaphore_signal(barrier, inc=1, device_id=to, device_id_type=MESH)
+
+    @pl.when(other_place)
+    def _():
+        for side in neighbours():
+            for to in side:
+                greet(to)
+        greet(device(core, 0, across, gz))
+
+    @pl.when(first_place)
+    def _():
+        for side in neighbours():
+            for to in side:
+                greet(to)
+        for step in range(1, 8):
+            for flip in range(2):
+                greet(device((core + flip) % 2, step, across, gz))
+        for i, j in STEPS:
+            greet(device(core, place, (across + i) % 8, (gz + j) % 8))
+
     for copy in loads:
         copy.wait()
 
+    local = None
+    for part in range(16):
+        rows = pl.ds(96 + 8 * part, 8)
+        sound = jnp.sqrt(gamma_gas * raw_x[4, rows, :] / raw_x[0, rows, :])
+        speed = (
+            jnp.abs(raw_x[1, rows, :]) + jnp.abs(raw_x[2, rows, :]) + jnp.abs(raw_x[3, rows, :])
+        ) + 3.0 * sound
+        local = speed if local is None else jnp.maximum(local, speed)
+    tops[0] = jnp.max(local, axis=0, keepdims=True)
+
     def cells(raw, cell, direction, start, blocks):
         first, second, third = ORDER[direction]
 
         def body(block, carry):
             rows = pl.ds(pl.multiple_of(start + 8 * block, 8), 8)
-            values, sound = cell_values(
+            values = cell_values(
                 raw[0, rows, :],
                 raw[1 + first, rows, :],
                 raw[1 + second, rows, :],
@@ -229,12 +256,9 @@
             )
             for index, value in enumerate(values):
                 cell[index, rows, :] = value
-            speed = (
-                jnp.abs(values[VN]) + jnp.abs(values[VA]) + jnp.abs(values[VB]) + 3.0 * sound
-            )
-            return jnp.maximum(carry, speed)
-
-        return lax.fori_loop(0, blocks, body, jnp.zeros((8, 128), jnp.float32))
+            return carry
+
+        lax.fori_loop(0, blocks, body, 0)
 
     def faces(cell, flux, stride, start, blocks):
         def body(block, carry):
@@ -249,101 +273,151 @@
 
         lax.fori_loop(0, blocks, body, 0)
 
-    local = cells(raw_x, cell_x, 0, 96, 16)
-    tops[0] = jnp.max(local, axis=0, keepdims=True)
-
-    for field in range(5):
-        for x in range(4):
-            for part in range(4):
-                raw_y[field, pl.ds(16 + 32 * part + x, 8, stride=4), :] = raw_x[
-                    field, pl.ds(96 + 32 * x + 8 * part, 8), :
-                ]
-        raw_z[field, pl.ds(16, 128), :] = raw_x[field, pl.ds(96, 128), :].T
-
-    pl.semaphore_wait(barrier, len(greeted))
-
-    def send_tops(phase):
-        first = (0, 15, 22)[phase]
-        copies = []
-        for slot, device in enumerate(lines[phase]):
-            copies.append(
-                pltpu.make_async_remote_copy(
-                    src_ref=tops.at[phase],
-                    dst_ref=top_in.at[first + slot],
-                    send_sem=max_send.at[first + slot],
-                    recv_sem=max_recv.at[first + slot],
-                    device_id=device,
-                    device_id_type=MESH,
-                )
+    def relayout():
+        for field in range(5):
+            for x in range(4):
+                for part in range(4):
+                    raw_y[field, pl.ds(16 + 32 * part + x, 8, stride=4), :] = raw_x[
+                        field, pl.ds(96 + 32 * x + 8 * part, 8), :
+                    ]
+            raw_z[field, pl.ds(16, 128), :] = raw_x[field, pl.ds(96, 128), :].T
+        cells(raw_x, cell_x, 0, 96, 16)
+
+    def interior():
+        cells(raw_z, cell_z, 2, 16, 16)
+        cells(raw_y, cell_y, 1, 16, 16)
+        faces(cell_z, flux_z, 1, 24, 14)
+        faces(cell_y, flux_y, 4, 24, 13)
+
+    def top_copy(source, slot, sent, to):
+        return pltpu.make_async_remote_copy(
+            src_ref=tops.at[source],
+            dst_ref=top_in.at[slot],
+            send_sem=max_send.at[sent],
+            recv_sem=max_recv.at[slot],
+            device_id=to,
+            device_id_type=MESH,
+        )
+
+    def first_copy(flip):
+        return top_copy(
+            0, 2 * place + flip, flip, device((core + flip) % 2, 0, across, gz)
+        )
+
+    def plane_copies():
+        return [
+            top_copy(
+                1, PLANE + k, PLANE + k, device(core, place, (across + i) % 8, (gz + j) % 8)
             )
-        for copy in copies:
+            for k, (i, j) in enumerate(STEPS)
+        ]
+
+    def final_copies():
+        return [
+            top_copy(2, FINAL, 1 + step, device(core, step, across, gz)) for step in range(1, 8)
+        ]
+
+    def halo_copy(raw, source, target, size, slot, to):
+        return pltpu.make_async_remote_copy(
+            src_ref=raw.at[:, pl.ds(source, size)],
+            dst_ref=raw.at[:, pl.ds(target, size)],
+            send_sem=halo_send.at[slot],
+            recv_sem=halo_recv.at[slot],
+            device_id=to,
+            device_id_type=MESH,
+        )
+
+    (next_x, next_y, next_z), (last_x, last_y, last_z) = neighbours()
+    halo_z = [
+        halo_copy(raw_z, 136, 8, 8, 0, next_z),
+        halo_copy(raw_z, 16, 144, 8, 1, last_z),
+    ]
+    halo_y = [
+        halo_copy(raw_y, 128, 0, 16, 2, next_y),
+        halo_copy(raw_y, 16, 144, 16, 3, last_y),
+    ]
+    head_x = halo_copy(raw_x, 96, 224, 96, 4, last_x)
+    tail_x = [
+        halo_copy(raw_x, 128 + 32 * plane, 32 * plane, 32, 5 + plane, next_x)
+        for plane in (2, 1, 0)
+    ]
+
+    @pl.when(early)
+    def _():
+        relayout()
+        interior()
+
+    pl.semaphore_wait(barrier, jnp.where(first_place, 6 + 7 + len(STEPS), 6 + 2))
+
+    @pl.when(other_place)
+    def _():
+        for flip in range(2):
+            first_copy(flip).start()
+
+    @pl.when(first_place)
+    def _():
+        first_copy(1).start()
+
+    for copy in tail_x:
+        copy.start()
+    held = jnp.logical_and(first_place, core == 0)
+
+    @pl.when(jnp.logical_not(held))
+    def _():
+        head_x.start()
+
+    @pl.when(jnp.logical_not(early))
+    def _():
+        relayout()
+
+    for copy in halo_z:
+        copy.start()
+
+    @pl.when(early)
+    def _():
+        for copy in halo_y:
             copy.start()
-        return copies
-
-    def gather_tops(phase, copies):
-        first = (0, 15, 22)[phase]
-        for copy in copies:
-            copy.wait()
-        top = tops[phase]
-        for slot in range(len(copies)):
-            top = jnp.maximum(top, top_in[first + slot])
-        return top
-
-    top_copies = send_tops(0)
-
-    def send_halos(direction):
-        raw, tail, tail_to, head, head_to, size = (
-            (raw_x, 128, 0, 96, 224, 96),
-            (raw_y, 128, 0, 16, 144, 16),
-            (raw_z, 136, 8, 16, 144, 8),
-        )[direction]
-        copies = []
-        for side, (source, target) in enumerate(((tail, tail_to), (head, head_to))):
-            copies.append(
-                pltpu.make_async_remote_copy(
-                    src_ref=raw.at[:, pl.ds(source, size)],
-                    dst_ref=raw.at[:, pl.ds(target, size)],
-                    send_sem=halo_send.at[2 * direction + side],
-                    recv_sem=halo_recv.at[2 * direction + side],
-                    device_id=halos[side][direction],
-                    device_id_type=MESH,
-                )
-            )
-        for copy in copies:
+
+    @pl.when(jnp.logical_not(early))
+    def _():
+        interior()
+        for copy in halo_y:
             copy.start()
-        return copies
-
-    halo_z = send_halos(2)
-    halo_y = send_halos(1)
-    halo_x = send_halos(0)
-
-    cells(raw_z, cell_z, 2, 16, 16)
-    cells(raw_y, cell_y, 1, 16, 16)
+
+    @pl.when(first_place)
+    def _():
+        for slot in range(1, 16):
+            top_copy(0, slot, 0, device(core, place, across, gz)).wait_recv()
+        top = tops[0]
+        for slot in range(1, 16):
+            top = jnp.maximum(top, top_in[slot])
+        tops[1] = top
+        for copy in plane_copies():
+            copy.start()
+
+    @pl.when(held)
+    def _():
+        head_x.start()
 
     for copy in halo_z:
-        copy.wait()
+        copy.wait_recv()
     cells(raw_z, cell_z, 2, 8, 1)
     cells(raw_z, cell_z, 2, 144, 1)
-    faces(cell_z, flux_z, 1, 8, 17)
-
-    tops[1] = gather_tops(0, top_copies)
-    top_copies = send_tops(1)
-
+    faces(cell_z, flux_z, 1, 8, 2)
+    faces(cell_z, flux_z, 1, 136, 1)
     for copy in halo_y:
-        copy.wait()
+        copy.wait_recv()
     cells(raw_y, cell_y, 1, 0, 2)
     cells(raw_y, cell_y, 1, 144, 2)
-    faces(cell_y, flux_y, 4, 8, 17)
-
-    tops[2] = gather_tops(1, top_copies)
-    top_copies = send_tops(2)
+    faces(cell_y, flux_y, 4, 8, 2)
+    faces(cell_y, flux_y, 4, 128, 2)
 
     for comp in range(5):
-        along_z = flux_z[comp_at(2, comp), pl.ds(16, 128), :] - flux_z[
-            comp_at(2, comp), pl.ds(15, 128), :
-        ]
-        total[comp] = along_z.T
+        along_z = comp_at(2, comp)
         along_y = comp_at(1, comp)
+        total[comp] = (
+            flux_z[along_z, pl.ds(16, 128), :] - flux_z[along_z, pl.ds(15, 128), :]
+        ).T
         for part in range(16):
             rows = pl.ds(16 + 8 * part, 8)
             flux_x[0, rows, :] = (
@@ -357,22 +431,58 @@
                     + flux_x[0, pl.ds(16 + 32 * part + x, 8, stride=4), :]
                 )
 
-    for copy in halo_x:
-        copy.wait()
-    cells(raw_x, cell_x, 0, 0, 12)
+    head_x.wait_recv()
     cells(raw_x, cell_x, 0, 224, 12)
-    faces(cell_x, flux_x, 32, 64, 20)
-
-    top = gather_tops(2, top_copies)
+    faces(cell_x, flux_x, 32, 160, 8)
+    for copy, plane in zip(tail_x, (2, 1, 0)):
+        copy.wait_recv()
+        cells(raw_x, cell_x, 0, 32 * plane, 4)
+        faces(cell_x, flux_x, 32, 64 + 32 * plane, 4)
+    for comp in range(5):
+        for part in range(16):
+            rows = pl.ds(8 * part, 8)
+            total[comp, rows, :] = total[comp, rows, :] + (
+                flux_x[comp, pl.ds(96 + 8 * part, 8), :]
+                - flux_x[comp, pl.ds(64 + 8 * part, 8), :]
+            )
+
+    @pl.when(first_place)
+    def _():
+        top = tops[1]
+        for copy in plane_copies():
+            copy.wait_recv()
+        for k in range(len(STEPS)):
+            top = jnp.maximum(top, top_in[PLANE + k])
+        tops[2] = top
+        for copy in final_copies():
+            copy.start()
+
+    @pl.when(other_place)
+    def _():
+        top_copy(2, FINAL, 0, device(core, 0, across, gz)).wait_recv()
+        tops[2] = top_in[FINAL]
+
+    top = tops[2]
     step = (cfl_number / 12.0) / jnp.max(top, axis=1, keepdims=True)
     for comp in range(5):
         for part in range(16):
             rows = pl.ds(8 * part, 8)
-            change = total[comp, rows, :] + (
-                flux_x[comp, pl.ds(96 + 8 * part, 8), :]
-                - flux_x[comp, pl.ds(64 + 8 * part, 8), :]
+            out_ref[comp, rows, :] = (
+                cell_x[comp, pl.ds(96 + 8 * part, 8), :] - step * total[comp, rows, :]
             )
-            out_ref[comp, rows, :] = cell_x[comp, pl.ds(96 + 8 * part, 8), :] - step * change
+    for copy in halo_z + halo_y + tail_x + [head_x]:
+        copy.wait_send()
+
+    @pl.when(other_place)
+    def _():
+        for flip in range(2):
+            first_copy(flip).wait_send()
+
+    @pl.when(first_place)
+    def _():
+        first_copy(1).wait_send()
+        for copy in plane_copies() + final_copies():
+            copy.wait_send()
 
 
 def comp_at(direction, comp):
@@ -386,7 +496,7 @@
     result = pl.pallas_call(
         kernel,
         name="section",
-        out_shape=jax.ShapeDtypeStruct((5, 128, 128), f32),
+        out_shape=pltpu.VMEM((5, 128, 128), f32),
         in_specs=[pl.BlockSpec(memory_space=pltpu.HBM)] * 3,
         out_specs=pl.BlockSpec(memory_space=pltpu.VMEM),
         scratch_shapes=[
@@ -401,12 +511,12 @@
             pltpu.VMEM((5, 144, 128), f32),
             pltpu.VMEM((5, 128, 128), f32),
             pltpu.VMEM((3, 1, 128), f32),
-            pltpu.VMEM((29, 1, 128), f32),
+            pltpu.VMEM((FINAL + 1, 1, 128), f32),
             pltpu.SemaphoreType.DMA((5,)),
-            pltpu.SemaphoreType.DMA((29,)),
-            pltpu.SemaphoreType.DMA((29,)),
-            pltpu.SemaphoreType.DMA((6,)),
-            pltpu.SemaphoreType.DMA((6,)),
+            pltpu.SemaphoreType.DMA((FINAL + 1,)),
+            pltpu.SemaphoreType.DMA((FINAL + 1,)),
+            pltpu.SemaphoreType.DMA((8,)),
+            pltpu.SemaphoreType.DMA((8,)),
         ],
         compiler_params=pltpu.CompilerParams(collective_id=0, has_side_effects=True),
     )(

time: 41.1 us -> 38.5 us (0.937)
  the two profiles are of different devices: /device:TPU:2 before, /device:TPU:16 now
where the time goes in v2:
time: 38.5 us; the launch traced here: 38.3 us
  Pallas kernels  37.6 us (98%)
  local copies, waits for them, and re-layouts  0.73 us (2%)
    pallas_call x1, Pallas kernels, local(): pl.pallas_call(kernel, name='section', out_shape=pltpu.VMEM((5, 128, 128)...  37.6 us

profile of v2, /device:TPU:16, one launch (start us, length us, event | category | flops | bytes accessed | tf_op | source)
XLA Modules:
  0.0 38.3 jit_solution(9312087558161205996)
XLA Ops:
  0.0 37.6 %section.1 = f32[5,128,128]{2,1,0:T(8,128)S(1)} custom-call(f32[128,128]{1,0:T(8,128)} %bitcast.6, f32[3,128,128]{2,1,0:T(8,128)} %bitcast.5, f32[128,128]{1,0:T(8,128)} %bitcast.7), custom_call_target="tpu_custom_call" | custom-call | tf_op jit(solution)/shard_map/section/pallas_call | solution.py:496
  37.6 0.7 %copy.5 = f32[5,4,32,128]{3,2,1,0:T(8,128)} copy(f32[5,4,32,128]{3,2,1,0:T(8,128)S(1)} %bitcast.4) | data formatting | bytes 655360
